TPU v7x, 32 devices: a whole 2x2x4 slice. The times are simulated.
32 devices in a mesh: rep: 4 (over y, x), fsdp: 8 (over z, core).
Axes of the slice: x: 2, y: 2, z: 4, core: 2. Of those that a mesh axis runs over, the one named last changes fastest.
Arguments:
- momentum: float32 [4, 18432, 2304], P('rep', 'fsdp'), may hold values from -60 to 60
- gradient: bfloat16 [4, 18432, 2304], P('rep', 'fsdp'), may hold values from -30 to 30
- right_factor: float32 [2304, 256], P('fsdp'), may hold values from -0.125 to 0.125
Outputs:
- new_momentum: float32 [4, 18432, 2304], P('rep', 'fsdp')
- update: bfloat16 [18432, 2304], P('fsdp')
- new_factor: float32 [2304, 256], P('fsdp')
All inputs are finite; a program needn't handle non-finite values.
Results may differ from a plain program's by a relative error of at most 0.001.
Values sent between devices are 32-bit elements; how exact they have to be, the bound alone decides.
A program may use at most 128 MiB of HBM per device.

v0:
```python
import math

import jax
import jax.numpy as jnp
from jax import lax
from jax.sharding import PartitionSpec as P

ROWS = 18432
COLS = 2304
RANK = 256


epsilon = 1e-06
decay_rate = 0.95
highest = lax.Precision.HIGHEST


def shards(momentum, gradient, right_factor):
    buffer = momentum[0] + gradient[0].astype(jnp.float32)
    replicas = lax.axis_size("rep")
    columns = buffer
    partial_left = jnp.dot(
        columns,
        lax.all_gather(right_factor, "fsdp", axis=0, tiled=True),
        precision=highest,
        preferred_element_type=jnp.float32,
    )
    projected = lax.psum(partial_left, "rep")
    local_gram = jnp.dot(
        projected.T, projected, precision=highest, preferred_element_type=jnp.float32
    )
    gram_matrix = lax.psum(local_gram, "fsdp")
    lower_factor = jnp.linalg.cholesky(gram_matrix)
    orthonormal = jax.scipy.linalg.solve_triangular(lower_factor, projected.T, lower=True).T
    columns = buffer
    scattered = lax.psum_scatter(
        lax.dot_general(
            columns,
            orthonormal,
            (((0,), (0,)), ((), ())),
            precision=highest,
            preferred_element_type=jnp.float32,
        ),
        "fsdp",
        scatter_dimension=0,
        tiled=True,
    )
    own_factor = lax.psum(scattered, "rep") / replicas
    full_factor = lax.all_gather(own_factor, "fsdp", axis=0, tiled=True)
    col_norms = jnp.sqrt(jnp.sum(full_factor * full_factor, axis=0) + epsilon)
    new_factor = own_factor / col_norms
    correction = lax.dot_general(
        orthonormal,
        full_factor,
        (((1,), (1,)), ((), ())),
        precision=highest,
        preferred_element_type=jnp.float32,
    )
    new_momentum = (buffer - (1.0 - decay_rate) * correction)[None]
    direction = lax.dot_general(
        orthonormal,
        full_factor / col_norms,
        (((1,), (1,)), ((), ())),
        precision=highest,
        preferred_element_type=jnp.float32,
    )
    update = (math.sqrt(ROWS * COLS / RANK) * direction).astype(jnp.bfloat16)
    return (new_momentum, update, new_factor)


def solution(mesh):
    in_specs = (P("rep", "fsdp", None), P("rep", "fsdp", None), P("fsdp", None))
    out_specs = (P("rep", "fsdp", None), P("fsdp", None), P("fsdp", None))
    return jax.shard_map(shards, mesh=mesh, in_specs=in_specs, out_specs=out_specs, check_vma=False)
```

profile of v0, /device:TPU:0, one launch (start us, length us, event | category | flops | bytes accessed | tf_op | source)
XLA Modules:
  0.0 512.4 jit_solution(980822565762107197)
XLA Ops:
  7.2 0.7 all-gather.3.cloned.1.call-update
  7.9 35.9 %all-gather.3.cloned.1.call-done = f32[2304,256]{1,0:T(8,128)} async-done(((f32[288,256]{1,0:T(8,128)}), f32[2304,256]{1,0:T(8,128)}) %all-gather.3.cloned.1.call-update) | async-done | bytes 2359312 | tf_op jit(solution)/shard_map/all_gather | solution.py:24
  43.8 22.8 %fusion.3 = f32[2304,256]{1,0:T(8,128)} fusion(f32[2304,256]{1,0:T(8,128)} %all-gather.3.cloned.1.call-done, f32[1,2304,2304]{2,1,0:T(8,128)} %param.3, bf16[1,2304,2304]{2,1,0:T(8,128)(2,1)} %param.4), kind=kOutput, calls=%fused_computation.7 | convolution fusion | flops 16318070784 | bytes 36569088 | tf_op jit(solution)/shard_map/dot_general | solution.py:22
  66.7 73.2 %all-reduce.5.cloned.1.call-done = f32[2304,256]{1,0:T(8,128)} async-done(((f32[2304,256]{1,0:T(8,128)}), f32[2304,256]{1,0:T(8,128)}) %all-reduce.5.cloned.1.call-update) | async-done | bytes 2359312 | tf_op jit(solution)/shard_map/psum | solution.py:28
  139.9 6.9 %fusion.21 = f32[256,256]{0,1:T(8,128)} fusion(f32[2304,256]{1,0:T(8,128)} %all-reduce.5.cloned.1.call-done), kind=kOutput, calls=%fused_computation.48 | convolution fusion | flops 1811939328 | bytes 2621440 | tf_op jit(solution)/shard_map/dot_general | solution.py:29
  146.9 0.3 reduce-scatter.2.cloned.1.call-start
  147.1 55.3 %all-reduce.7.cloned.1.call-done = f32[256,256]{0,1:T(8,128)} async-done(((f32[256,256]{0,1:T(8,128)}), f32[256,256]{0,1:T(8,128)}) %all-reduce.7.cloned.1.call-update) | async-done | bytes 262160 | tf_op jit(solution)/shard_map/psum | solution.py:32
  202.4 1.1 copy.7
  203.5 1.0 fusion.11
  204.5 11.7 %cholesky.50 = f32[128,128]{1,0:T(8,128)S(1)} custom-call(f32[128,128]{1,0:T(8,128)S(1)} %cholesky.118), custom_call_target="Cholesky" | custom-call | tf_op jit(solution)/shard_map/jit(cholesky)/cholesky | solution.py:33
  216.3 9.8 %custom-call.15 = f32[1,128,128]{1,2,0:T(8,128)S(1)} custom-call(f32[1,128,128]{2,1,0:T(8,128)S(1)} %get-tuple-element.24), custom_call_target="InvertDiagBlocksLowerTriangular" | custom-call | tf_op jit(solution)/shard_map/jit(cholesky)/cholesky | solution.py:33
  226.3 0.3 convolution_subtract_fusion.1
  226.6 11.7 %cholesky.105 = f32[128,128]{1,0:T(8,128)S(1)} custom-call(f32[128,128]{1,0:T(8,128)S(1)} %convolution_subtract_fusion.1), custom_call_target="Cholesky" | custom-call | tf_op jit(solution)/shard_map/jit(cholesky)/cholesky | solution.py:33
  238.3 0.6 compare_reduce_fusion
  240.4 4.4 while.1
  240.8 0.6 fusion.31
  241.4 1.4 bitcast_dynamic-update-slice_fusion.2
  242.8 0.6 fusion.31
  243.4 1.4 bitcast_dynamic-update-slice_fusion.2
  244.8 20.3 %custom-call.16 = f32[2,128,128]{1,2,0:T(8,128)} custom-call(f32[2,128,128]{2,1,0:T(8,128)S(1)} %get-tuple-element.10), custom_call_target="InvertDiagBlocksLowerTriangular" | custom-call | tf_op jit(solution)/shard_map/jit(_solve_triangular)/triangular_solve | solution.py:34
  265.1 2.0 fusion.8
  267.1 2.9 convolution_subtract_fusion
  270.0 1.2 fusion.13
  271.2 38.5 %fusion.1 = f32[2304,256]{1,0:T(8,128)} fusion(f32[1,2304,2304]{2,1,0:T(8,128)} %param.3, bf16[1,2304,2304]{2,1,0:T(8,128)(2,1)} %param.4, f32[128,2304]{1,0:T(8,128)S(1)} %fusion.13, f32[128,2304]{1,0:T(8,128)S(1)} %fusion.8), kind=kOutput, calls=%fused_computation.5 | convolution fusion | flops 16318660608 | bytes 36569088 | tf_op jit(solution)/shard_map/dot_general | solution.py:37
  309.7 36.2 %reduce-scatter.2.cloned.1.call-done = f32[288,256]{1,0:T(8,128)} async-done(((f32[2304,256]{1,0:T(8,128)}), f32[288,256]{1,0:T(8,128)}) %reduce-scatter.2.cloned.1.call-update) | async-done | bytes 294928 | tf_op jit(solution)/shard_map/reduce_scatter | solution.py:36
  346.0 45.0 %all-reduce.9.cloned.1.call-done = f32[288,256]{1,0:T(8,128)} async-done(((f32[288,256]{1,0:T(8,128)}), f32[288,256]{1,0:T(8,128)}) %all-reduce.9.cloned.1.call-update) | async-done | bytes 294928 | tf_op jit(solution)/shard_map/psum | solution.py:48
  391.0 1.8 broadcast_multiply_fusion
  392.8 31.8 %all-gather.5.cloned.1.call-done = f32[2304,256]{1,0:T(8,128)} async-done(((f32[288,256]{1,0:T(8,128)}), f32[2304,256]{1,0:T(8,128)}) %all-gather.5.cloned.1.call-update) | async-done | bytes 2359312 | tf_op jit(solution)/shard_map/all_gather | solution.py:49
  424.5 2.1 multiply_reduce_fusion
  426.7 0.7 broadcast_divide_fusion
  427.4 36.8 %fusion.6 = bf16[2304,2304]{1,0:T(8,128)(2,1)} fusion(f32[2304,256]{1,0:T(8,128)} %all-gather.5.cloned.1.call-done, f32[128,2304]{1,0:T(8,128)S(1)} %fusion.13, f32[128,2304]{1,0:T(8,128)S(1)} %fusion.8, f32[256]{0:T(256)S(1)} %add_sqrt_fusion), kind=kOutput, calls=%fused_computation.11 | convolution fusion | flops 16319250432 | bytes 15336448 | tf_op jit(solution)/shard_map/dot_general | solution.py:60
  464.3 40.8 %fusion.5 = f32[1,2304,2304]{2,1,0:T(8,128)} fusion(f32[2304,256]{1,0:T(8,128)} %all-gather.5.cloned.1.call-done, f32[1,2304,2304]{2,1,0:T(8,128)} %param.3, bf16[1,2304,2304]{2,1,0:T(8,128)(2,1)S(1)} %bitcast.47, f32[128,2304]{1,0:T(8,128)S(1)} %fusion.13, f32[128,2304]{1,0:T(8,128)S(1)} %fusion.8), kind=kOutput, calls=%fused_computation.10 | convolution fusion | flops 16329277440 | bytes 57802752 | tf_op jit(solution)/shard_map/dot_general | solution.py:52
  (37 shorter events, 0.7 us)
Async XLA Ops:
  7.2 36.6 %all-gather.3.cloned.1.call-start = ((), (), s32[]{:S(2)}) async-start(), calls=%async_computation.1 | async-start | bytes 2654208 | tf_op jit(solution)/shard_map/all_gather | solution.py:24
  7.9 132.0 %all-reduce.5.cloned.1.call-start = ((), (), s32[]{:S(2)}) async-start(), calls=%async_computation.2 | async-start | bytes 4718592 | tf_op jit(solution)/shard_map/psum | solution.py:28
  66.6 135.8 %all-reduce.7.cloned.1.call-start = ((), (), s32[]{:S(2)}) async-start(), calls=%async_computation.3 | async-start | bytes 524288 | tf_op jit(solution)/shard_map/psum | solution.py:32
  146.8 118.3 %copy-start = (f32[2304,256]{1,0:T(8,128)S(1)}, f32[2304,256]{1,0:T(8,128)}, u32[]{:S(2)}) copy-start(f32[2304,256]{1,0:T(8,128)} %all-reduce.5.cloned.1.call-done) | copy-start | bytes 7077892
  146.9 199.1 %reduce-scatter.2.cloned.1.call-start = ((), (), s32[]{:S(2)}) async-start(), calls=%async_computation.4 | async-start | bytes 2654208 | tf_op jit(solution)/shard_map/reduce_scatter | solution.py:36
  244.8 20.3 %copy-start.1 = (f32[256,256]{1,0:T(8,128)}, f32[256,256]{1,0:T(8,128)S(1)}, u32[]{:S(2)}) copy-start(f32[256,256]{1,0:T(8,128)S(1)} %get-tuple-element.86) | copy-start | bytes 786436
  267.1 2.9 copy-start.3
  309.7 81.3 %all-reduce.9.cloned.1.call-start = ((), (), s32[]{:S(2)}) async-start(), calls=%async_computation.5 | async-start | bytes 589824 | tf_op jit(solution)/shard_map/psum | solution.py:48
  346.0 78.6 %all-gather.5.cloned.1.call-start = ((), (), s32[]{:S(2)}) async-start(), calls=%async_computation.6 | async-start | bytes 2654208 | tf_op jit(solution)/shard_map/all_gather | solution.py:49
  391.0 35.7 %copy-start.2 = (f32[288,256]{1,0:T(8,128)S(1)}, f32[288,256]{1,0:T(8,128)}, u32[]{:S(2)}) copy-start(f32[288,256]{1,0:T(8,128)} %all-reduce.9.cloned.1.call-done) | copy-start | bytes 884740
  424.5 39.7 %slice-start = ((s8[10616832]{0:T(1024)(128)(4,1)}), s8[4194304]{0:T(1024)(128)(4,1)S(1)}, s32[]{:S(2)}) async-start(s8[10616832]{0:T(1024)(128)(4,1)} %bitcast.46), calls=%async_computation.7 | async-start | bytes 8388608
  427.4 36.8 %slice-start.1 = ((s8[10616832]{0:T(1024)(128)(4,1)}), s8[4194304]{0:T(1024)(128)(4,1)S(1)}, s32[]{:S(2)}) async-start(s8[10616832]{0:T(1024)(128)(4,1)} %bitcast.46), calls=%async_computation.8 | async-start | bytes 8388608
  427.4 36.8 %slice-start.2 = ((s8[10616832]{0:T(1024)(128)(4,1)}), s8[2228224]{0:T(1024)(128)(4,1)S(1)}, s32[]{:S(2)}) async-start(s8[10616832]{0:T(1024)(128)(4,1)} %bitcast.46), calls=%async_computation.9 | async-start | bytes 4456448
Sparse Core Ops, SparseCore 0:
  9.6 34.1 all-gather.2
  66.8 73.0 all-reduce.4
  147.0 55.4 all-reduce.6
  309.8 36.0 reduce-scatter.1
  348.7 42.2 all-reduce.8
  393.1 31.4 all-gather.4
where the time goes:
time: 520 us; the launch traced here: 512 us
  waiting for transfers between devices  278 us (53%)
  matrix products  152 us (29%)
  other arithmetic  59.9 us (12%)
  between operations  16 us (3%)
    psum x1, waiting for transfers between devices, shards(): projected = lax.psum(partial_left, 'rep')  73.2 us
    psum x1, waiting for transfers between devices, shards(): gram_matrix = lax.psum(local_gram, 'fsdp')  55.3 us
    psum x1, waiting for transfers between devices, shards(): own_factor = lax.psum(scattered, 'rep') / replicas  45 us
    dot_general x1, matrix products, shards(): lax.dot_general(orthonormal, full_factor, (((1,), (1,)), ((), ())), preci...  40.8 us
    dot_general x1, matrix products, shards(): lax.dot_general(columns, orthonormal, (((0,), (0,)), ((), ())), precision...  38.5 us
    dot_general x1, matrix products, shards(): lax.dot_general(orthonormal, full_factor / col_norms, (((1,), (1,)), ((),...  36.8 us
    reduce_scatter x1, waiting for transfers between devices, shards(): lax.psum_scatter(lax.dot_general(columns, orthonormal, (((0,), (0,)), (()...  36.2 us
    all_gather x1, waiting for transfers between devices, shards(): lax.all_gather(right_factor, 'fsdp', axis=0, tiled=True)  35.9 us
  transfers between devices with their start and end apart: 6, of which 6 were waited for; matrix products, arithmetic and copies ran while one was open for 0% of the time, Pallas kernels for 0%

commit v1 on v0

v1 whole, which is shorter than its diff:
```python
import functools
import math

import jax
import jax.numpy as jnp
from jax import lax
from jax.experimental import pallas as pl
from jax.experimental.pallas import tpu as pltpu
from jax.sharding import PartitionSpec as P

epsilon = 1e-06
decay_rate = 0.95
highest = lax.Precision.HIGHEST
f32 = jnp.float32
bf16 = jnp.bfloat16
MESH = pl.DeviceIdType.MESH
VMEM_LIMIT = 60 * 1024 * 1024


def split(x):
    high = x.astype(bf16)
    return high, (x - high.astype(f32)).astype(bf16)


def dot(a, b, dims=(((1,), (0,)), ((), ()))):
    return lax.dot_general(a, b, dims, preferred_element_type=f32)


def exact(a, b, dims=(((1,), (0,)), ((), ()))):
    return lax.dot_general(a, b, dims, precision=highest, preferred_element_type=f32)


NT = (((1,), (1,)), ((), ()))
TN = (((0,), (0,)), ((), ()))


def greet(peers):
    barrier = pltpu.get_barrier_semaphore()
    for peer in peers:
        pl.semaphore_signal(barrier, inc=1, device_id=peer, device_id_type=MESH)
    pl.semaphore_wait(barrier, len(peers))


def remote(src, dst, send_sem, recv_sem, peer):
    copy = pltpu.make_async_remote_copy(
        src_ref=src, dst_ref=dst, send_sem=send_sem, recv_sem=recv_sem,
        device_id=peer, device_id_type=MESH,
    )
    copy.start()
    return copy


def gather_right(shard_n, own_ref, full_ref, send, recv, fsend, frecv, local):
    f = lax.axis_index("fsdp")
    r = lax.axis_index("rep")
    rows = own_ref.shape[0]
    chips = shard_n // 2
    chip, core = f // 2, lax.rem(f, 2)
    mate = (r, chip * 2 + 1 - core)
    others = [(r, lax.rem(chip + k, chips) * 2 + core) for k in range(1, chips)]
    greet([mate] + others)

    def block(index):
        return full_ref.at[pl.ds(pl.multiple_of(index * rows, 8), rows)]

    own = pltpu.make_async_copy(own_ref, block(f), local)
    own.start()
    copies = [remote(own_ref, block(f), send.at[k], recv.at[k], others[k]) for k in range(chips - 1)]
    passed = [remote(own_ref, block(f), fsend.at[0], frecv.at[0], mate)]
    for k in reversed(range(chips - 1)):
        copies[k].wait_recv()
        source = lax.rem(chip - (k + 1) + chips, chips) * 2 + core
        passed.append(remote(block(source), block(source), fsend.at[k + 1], frecv.at[k + 1], mate))
    for copy in copies:
        copy.wait_send()
    for copy in passed:
        copy.wait()
    own.wait()


def project(m_ref, g_ref, right_ref, out_ref, high, low):
    @pl.when(pl.program_id(0) == 0)
    def _():
        high[...], low[...] = split(right_ref[...])

    bh, bl = split(m_ref[0] + g_ref[0].astype(f32))
    out_ref[...] = dot(bh, high[...]) + dot(bh, low[...]) + dot(bl, high[...])


def inverse_small(a, size):
    row = lax.broadcasted_iota(jnp.int32, (size, 2 * size), 0)
    lane = lax.broadcasted_iota(jnp.int32, (size, 2 * size), 1)
    eye = jnp.where(row == lane - size, 1.0, 0.0).astype(f32)
    work = jnp.concatenate([a, eye[:, size:]], axis=1)
    for j in range(size):
        first = (j // 8) * 8
        pivot = work[j:j + 1, :]
        scaled = pivot / work[j:j + 1, j:j + 1]
        tail = work[first:, :]
        below = row[first:, :] > j
        tail = tail - jnp.where(below, tail[:, j:j + 1], 0.0) * scaled
        work = tail if first == 0 else jnp.concatenate([work[:first], tail], axis=0)
    diag = jnp.sum(jnp.where(row == lane, work, 0.0), axis=1, keepdims=True)
    return work[:, size:] * (1.0 / jnp.sqrt(diag))


def inverse_lower(a, size):
    if size <= 64:
        return inverse_small(a, size)
    h = size // 2
    top = inverse_lower(a[:h, :h], h)
    cross = exact(a[h:, :h], top, NT)
    low = inverse_lower(a[h:, h:] - exact(cross, cross, NT), h)
    corner = -exact(low, exact(cross, top))
    return jnp.concatenate(
        [jnp.concatenate([top, jnp.zeros((h, h), f32)], axis=1),
         jnp.concatenate([corner, low], axis=1)], axis=0)


def orthonormalize(reps, shard_n, part_ref, q_ref, full, xin, yin, xin2, yin2, gout, gin, gfull, inv,
                   send, recv, gsend, grecv, asend, arecv):
    r = lax.axis_index("rep")
    f = lax.axis_index("fsdp")
    rows, rank = part_ref.shape
    chunk = rows // reps
    half = rank // 2
    total = reps * shard_n
    me = r * shard_n + f
    sx = 1 - 2 * lax.rem(r, 2)
    sy = 1 - 2 * (r // 2)
    px, py, pd = r + sx, r + 2 * sy, r + sx + 2 * sy
    left, right = pl.ds(0, half), pl.ds(half, half)

    def of(index):
        return pl.ds(pl.multiple_of(index * chunk, 8), chunk)

    def device(k):
        d = lax.rem(me + k, total)
        return d, (d // shard_n, lax.rem(d, shard_n))

    peers = [device(k) for k in range(1, total)]
    greet([peer for _, peer in peers])

    s1 = [
        remote(part_ref.at[of(pd), left], xin.at[0], send.at[0], recv.at[0], (px, f)),
        remote(part_ref.at[of(pd), right], yin.at[0], send.at[1], recv.at[1], (py, f)),
        remote(part_ref.at[of(px), left], xin.at[1], send.at[2], recv.at[2], (px, f)),
        remote(part_ref.at[of(py), right], yin.at[1], send.at[3], recv.at[3], (py, f)),
    ]
    s1[0].wait_recv()
    xin[0] = xin[0] + part_ref[of(py), left]
    a = remote(xin.at[0], xin2, send.at[4], recv.at[4], (py, f))
    s1[1].wait_recv()
    yin[0] = yin[0] + part_ref[of(px), right]
    b = remote(yin.at[0], yin2, send.at[5], recv.at[5], (px, f))
    s1[2].wait_recv()
    xin[1] = xin[1] + part_ref[of(r), left]
    s1[3].wait_recv()
    yin[1] = yin[1] + part_ref[of(r), right]
    a.wait_recv()
    full[of(r), left] = xin[1] + xin2[...]
    b.wait_recv()
    full[of(r), right] = yin[1] + yin2[...]

    own = full[of(r), :]
    piece = rank // total
    gout[...] = exact(own, own, TN)

    def rows_of(index):
        return pl.ds(pl.multiple_of(index * piece, 8), piece)

    g1 = [
        remote(gout.at[rows_of(d)], gin.at[k], gsend.at[k], grecv.at[k], peer)
        for k, (d, peer) in enumerate(peers)
    ]
    acc = gout[rows_of(me), :]
    for k in range(total - 1):
        g1[k].wait_recv()
        acc = acc + gin[k]
    gfull[rows_of(me), :] = acc
    g2 = [
        remote(gfull.at[rows_of(me)], gfull.at[rows_of(me)], asend.at[k], arecv.at[k], peer)
        for k, (d, peer) in enumerate(peers)
    ]
    t1 = [
        remote(full.at[of(r), left], full.at[of(r), left], send.at[6], recv.at[6], (px, f)),
        remote(full.at[of(r), right], full.at[of(r), right], send.at[7], recv.at[7], (py, f)),
        remote(full.at[of(r), right], full.at[of(r), right], send.at[8], recv.at[8], (px, f)),
        remote(full.at[of(r), left], full.at[of(r), left], send.at[9], recv.at[9], (py, f)),
    ]
    for copy in g2:
        copy.wait_recv()
    t1[0].wait_recv()
    t2 = [remote(full.at[of(px), left], full.at[of(px), left], send.at[10], recv.at[10], (py, f))]
    t1[1].wait_recv()
    t2.append(remote(full.at[of(py), right], full.at[of(py), right], send.at[11], recv.at[11], (px, f)))
    inv[...] = inverse_lower(gfull[...], rank)
    t1[2].wait_recv()
    t1[3].wait_recv()
    t2[0].wait_recv()
    t2[1].wait_recv()
    for copy in s1 + [a, b] + g1 + g2 + t1 + t2:
        copy.wait_send()
    step = 256 if rows % 256 == 0 else chunk

    @pl.loop(0, rows // step)
    def _(i):
        at = pl.ds(pl.multiple_of(i * step, 8), step)
        q_ref[at, :] = exact(full[at, :], inv[...], NT)


def factor_term(m_ref, g_ref, q_ref, out_ref):
    bh, bl = split(m_ref[0] + g_ref[0].astype(f32))
    qh, ql = split(q_ref[...].T)
    term = dot(qh, bh) + dot(qh, bl) + dot(ql, bh)

    @pl.when(pl.program_id(0) == 0)
    def _():
        out_ref[...] = term

    @pl.when(pl.program_id(0) != 0)
    def _():
        out_ref[...] += term


def sum_factor(reps, shard_n, part_ref, out_ref, cin, xin, yin, xin2, yin2, zin, zsum, send, recv, zsend, zrecv):
    r = lax.axis_index("rep")
    f = lax.axis_index("fsdp")
    chips = shard_n // 2
    chip, core = f // 2, lax.rem(f, 2)
    rank, cols = part_ref.shape
    half = cols // 2
    left, right = pl.ds(0, half), pl.ds(half, half)
    sx = 1 - 2 * lax.rem(r, 2)
    sy = 1 - 2 * (r // 2)
    px, py, pd = r + sx, r + 2 * sy, r + sx + 2 * sy
    n0 = rank // 2
    n1 = n0 // reps
    n2 = n1 // chips
    mate = (r, chip * 2 + 1 - core)
    zs = [lax.rem(chip + k, chips) for k in range(1, chips)]
    greet([mate, (px, f), (py, f)] + [(r, z * 2 + core) for z in zs])

    def of(index):
        return pl.ds(pl.multiple_of(index * n1, 8), n1)

    mine = core * n0
    order = [pd, px, py, r]
    c = []
    for k, which in enumerate(order):
        away = pl.ds(pl.multiple_of((1 - core) * n0 + which * n1, 8), n1)
        c.append(remote(part_ref.at[away], cin.at[of(which)], send.at[k], recv.at[k], mate))

    def add_own(which):
        at = pl.ds(pl.multiple_of(mine + which * n1, 8), n1)
        cin[of(which), :] = cin[of(which), :] + part_ref[at, :]

    c[0].wait_recv()
    add_own(pd)
    s1 = [
        remote(cin.at[of(pd), left], xin.at[0], send.at[4], recv.at[4], (px, f)),
        remote(cin.at[of(pd), right], yin.at[0], send.at[5], recv.at[5], (py, f)),
    ]
    c[1].wait_recv()
    add_own(px)
    s1.append(remote(cin.at[of(px), left], xin.at[1], send.at[6], recv.at[6], (px, f)))
    c[2].wait_recv()
    add_own(py)
    s1.append(remote(cin.at[of(py), right], yin.at[1], send.at[7], recv.at[7], (py, f)))
    c[3].wait_recv()
    add_own(r)
    s1[0].wait_recv()
    xin[0] = xin[0] + cin[of(py), left]
    a = remote(xin.at[0], xin2, send.at[8], recv.at[8], (py, f))
    s1[1].wait_recv()
    yin[0] = yin[0] + cin[of(px), right]
    b = remote(yin.at[0], yin2, send.at[9], recv.at[9], (px, f))
    s1[2].wait_recv()
    xin[1] = xin[1] + cin[of(r), left]
    s1[3].wait_recv()
    yin[1] = yin[1] + cin[of(r), right]
    a.wait_recv()
    zsum[:, left] = xin[1] + xin2[...]
    b.wait_recv()
    zsum[:, right] = yin[1] + yin2[...]
    z1 = []
    for k, z in enumerate(zs):
        rows = pl.ds(pl.multiple_of(z * n2, 8), n2)
        z1.append(remote(zsum.at[rows], zin.at[k], zsend.at[k], zrecv.at[k], (r, z * 2 + core)))
    acc = zsum[pl.ds(pl.multiple_of(chip * n2, 8), n2), :]
    for k in range(chips - 1):
        z1[k].wait_recv()
        acc = acc + zin[k]

    def block(rep, z, co):
        return pl.ds(pl.multiple_of(co * n0 + rep * n1 + z * n2, 8), n2)

    def group(rep, co):
        return pl.ds(pl.multiple_of(co * n0 + rep * n1, 8), n1)

    at = block(r, chip, core)
    out_ref[at, :] = acc * (1.0 / reps)
    z2 = [
        remote(out_ref.at[at], out_ref.at[at], zsend.at[chips + k], zrecv.at[chips + k], (r, z * 2 + core))
        for k, z in enumerate(zs)
    ]
    for copy in z2:
        copy.wait_recv()
    whole = group(r, core)
    t = [
        remote(out_ref.at[whole, left], out_ref.at[whole, left], send.at[10], recv.at[10], (px, f)),
        remote(out_ref.at[whole, right], out_ref.at[whole, right], send.at[11], recv.at[11], (py, f)),
        remote(out_ref.at[whole, right], out_ref.at[whole, right], send.at[12], recv.at[12], (px, f)),
        remote(out_ref.at[whole, left], out_ref.at[whole, left], send.at[13], recv.at[13], (py, f)),
        remote(out_ref.at[whole], out_ref.at[whole], send.at[14], recv.at[14], mate),
    ]
    t[0].wait_recv()
    gx, gy, gd = group(px, core), group(py, core), group(pd, core)
    t.append(remote(out_ref.at[gx, left], out_ref.at[gx, left], send.at[15], recv.at[15], (py, f)))
    t[1].wait_recv()
    t.append(remote(out_ref.at[gy, right], out_ref.at[gy, right], send.at[16], recv.at[16], (px, f)))
    t[2].wait_recv()
    t.append(remote(out_ref.at[gx], out_ref.at[gx], send.at[17], recv.at[17], mate))
    t[3].wait_recv()
    t.append(remote(out_ref.at[gy], out_ref.at[gy], send.at[18], recv.at[18], mate))
    t[5].wait_recv()
    t[6].wait_recv()
    t.append(remote(out_ref.at[gd], out_ref.at[gd], send.at[19], recv.at[19], mate))
    for index in (4, 7, 8, 9):
        t[index].wait_recv()
    for copy in c + s1 + [a, b] + z1 + z2 + t:
        copy.wait_send()


def finish(scale, m_ref, g_ref, q_ref, factor_ref, mom_ref, upd_ref, new_ref, plain, high, low):
    @pl.when(pl.program_id(0) == 0)
    def _():
        factor = factor_ref[...]
        norms = jnp.sqrt(jnp.sum(factor * factor, axis=1, keepdims=True) + epsilon)
        new = factor / norms
        new_ref[...] = new
        plain[...] = ((1.0 - decay_rate) * factor).astype(bf16)
        high[...], low[...] = split(new)

    qh, ql = split(q_ref[...])
    mom_ref[0] = (m_ref[0] + g_ref[0].astype(f32)) - dot(qh, plain[...])
    direction = dot(qh, high[...]) + dot(qh, low[...]) + dot(ql, high[...])
    upd_ref[...] = (scale * direction).astype(bf16)


def params(**more):
    return pltpu.CompilerParams(vmem_limit_bytes=VMEM_LIMIT, **more)


def by_kernels(reps, shard_n, total_rows, momentum, gradient, right_factor):
    _, rows, cols = momentum.shape
    rank = right_factor.shape[1]
    tile = 256 if rows % 256 == 0 else rows // 8
    steps = rows // tile
    vmem = pl.BlockSpec(memory_space=pltpu.VMEM)
    dma = pltpu.SemaphoreType.DMA
    chips = shard_n // 2

    def stripe(width):
        return pl.BlockSpec((tile, width), lambda i: (i, 0))

    cube = pl.BlockSpec((1, tile, cols), lambda i: (0, i, 0))

    def fixed(*shape):
        return pl.BlockSpec(shape, lambda i: (0,) * len(shape))

    right = pl.pallas_call(
        functools.partial(gather_right, shard_n),
        out_shape=jax.ShapeDtypeStruct((cols, rank), f32),
        in_specs=[vmem], out_specs=vmem,
        scratch_shapes=[dma((chips,)), dma((chips,)), dma((chips,)), dma((chips,)), dma],
        compiler_params=params(collective_id=0, has_side_effects=True),
        name="gather_right",
    )(right_factor)
    partial = pl.pallas_call(
        project,
        grid=(steps,),
        out_shape=jax.ShapeDtypeStruct((rows, rank), f32),
        in_specs=[cube, cube, fixed(cols, rank)], out_specs=stripe(rank),
        scratch_shapes=[pltpu.VMEM((cols, rank), bf16)] * 2,
        compiler_params=params(), name="project",
    )(momentum, gradient, right)
    chunk, total = rows // reps, reps * shard_n
    orthonormal = pl.pallas_call(
        functools.partial(orthonormalize, reps, shard_n),
        out_shape=jax.ShapeDtypeStruct((rows, rank), f32),
        in_specs=[vmem], out_specs=vmem,
        scratch_shapes=[
            pltpu.VMEM((rows, rank), f32),
            pltpu.VMEM((2, chunk, rank // 2), f32), pltpu.VMEM((2, chunk, rank // 2), f32),
            pltpu.VMEM((chunk, rank // 2), f32), pltpu.VMEM((chunk, rank // 2), f32),
            pltpu.VMEM((rank, rank), f32),
            pltpu.VMEM((total, rank // total, rank), f32),
            pltpu.VMEM((rank, rank), f32), pltpu.VMEM((rank, rank), f32),
            dma((12,)), dma((12,)), dma((total,)), dma((total,)), dma((total,)), dma((total,)),
        ],
        compiler_params=params(collective_id=1, has_side_effects=True),
        name="orthonormalize",
    )(partial)
    term = pl.pallas_call(
        factor_term,
        grid=(steps,),
        out_shape=jax.ShapeDtypeStruct((rank, cols), f32),
        in_specs=[cube, cube, stripe(rank)], out_specs=fixed(rank, cols),
        compiler_params=params(), name="factor_term",
    )(momentum, gradient, orthonormal)
    n1 = rank // 2 // reps
    factor = pl.pallas_call(
        functools.partial(sum_factor, reps, shard_n),
        out_shape=jax.ShapeDtypeStruct((rank, cols), f32),
        in_specs=[vmem], out_specs=vmem,
        scratch_shapes=[
            pltpu.VMEM((rank // 2, cols), f32),
            pltpu.VMEM((2, n1, cols // 2), f32), pltpu.VMEM((2, n1, cols // 2), f32),
            pltpu.VMEM((n1, cols // 2), f32), pltpu.VMEM((n1, cols // 2), f32),
            pltpu.VMEM((chips, n1 // chips, cols), f32), pltpu.VMEM((n1, cols), f32),
            dma((20,)), dma((20,)), dma((2 * chips,)), dma((2 * chips,)),
        ],
        compiler_params=params(collective_id=2, has_side_effects=True),
        name="sum_factor",
    )(term)
    new_momentum, update, new = pl.pallas_call(
        functools.partial(finish, math.sqrt(total_rows * cols / rank)),
        grid=(steps,),
        out_shape=(
            jax.ShapeDtypeStruct(momentum.shape, f32),
            jax.ShapeDtypeStruct((rows, cols), bf16),
            jax.ShapeDtypeStruct((rank, cols), f32),
        ),
        in_specs=[cube, cube, stripe(rank), fixed(rank, cols)],
        out_specs=(cube, stripe(cols), fixed(rank, cols)),
        scratch_shapes=[pltpu.VMEM((rank, cols), bf16)] * 3,
        compiler_params=params(), name="finish",
    )(momentum, gradient, orthonormal, factor)
    own = cols // shard_n
    new_factor = lax.dynamic_slice_in_dim(new, lax.axis_index("fsdp") * own, own, axis=1).T
    return new_momentum, update, new_factor


def by_collectives(reps, shard_n, total_rows, momentum, gradient, right_factor):
    buffer = momentum[0] + gradient[0].astype(f32)
    partial = exact(buffer, lax.all_gather(right_factor, "fsdp", axis=0, tiled=True))
    projected = lax.psum(partial, "rep")
    gram_matrix = lax.psum(exact(projected, projected, TN), "fsdp")
    lower_factor = jnp.linalg.cholesky(gram_matrix)
    orthonormal = jax.scipy.linalg.solve_triangular(lower_factor, projected.T, lower=True).T
    scattered = lax.psum_scatter(
        exact(buffer, orthonormal, TN), "fsdp", scatter_dimension=0, tiled=True)
    own_factor = lax.psum(scattered, "rep") / reps
    full_factor = lax.all_gather(own_factor, "fsdp", axis=0, tiled=True)
    col_norms = jnp.sqrt(jnp.sum(full_factor * full_factor, axis=0) + epsilon)
    new_factor = own_factor / col_norms
    correction = exact(orthonormal, full_factor, NT)
    new_momentum = (buffer - (1.0 - decay_rate) * correction)[None]
    direction = exact(orthonormal, full_factor / col_norms, NT)
    scale = math.sqrt(total_rows * buffer.shape[1] / right_factor.shape[1])
    return new_momentum, (scale * direction).astype(bf16), new_factor


def solution(mesh):
    reps, shard_n = mesh.shape["rep"], mesh.shape["fsdp"]

    def shards(momentum, gradient, right_factor):
        rows, cols = momentum.shape[1:]
        rank = right_factor.shape[1]
        fits = (
            reps == 4 and shard_n % 2 == 0 and shard_n > 2 and rows % 128 == 0
            and (cols // shard_n) % 8 == 0 and cols % 256 == 0
            and rank % (8 * reps * shard_n) == 0
        )
        run = by_kernels if fits else by_collectives
        return run(reps, shard_n, rows * shard_n, momentum, gradient, right_factor)

    in_specs = (P("rep", "fsdp", None), P("rep", "fsdp", None), P("fsdp", None))
    out_specs = (P("rep", "fsdp", None), P("fsdp", None), P("fsdp", None))
    return jax.shard_map(shards, mesh=mesh, in_specs=in_specs, out_specs=out_specs, check_vma=False)
```

time: 520 us -> 224 us (0.43); the launches traced: 512 us -> 223 us
  waiting for transfers between devices: 278 us -> 0 us
  Pallas kernels: 0 us -> 220 us
  matrix products: 152 us -> 0 us
  other arithmetic: 59.9 us -> 0 us
  between operations: 16 us -> 0.66 us
    pallas_call x0 -> x6, Pallas kernels: none -> 220 us  [the longest x1 83.2 us: by_kernels(): pl.pallas_call(functools.partial(orthonormalize, reps, shard_n), out_shap...]
    psum x3 -> x0, waiting for transfers between devices: 173 us -> none  [the longest x1 73.2 us: shards(): projected = lax.psum(partial_left, 'rep')]
    dot_general x5 -> x0, matrix products: 146 us -> none  [the longest x1 40.8 us: shards(): lax.dot_general(orthonormal, full_factor, (((1,), (1,)), ((), ())), preci...]
    all_gather x2 -> x0, waiting for transfers between devices: 67.6 us -> none  [the longest x1 35.9 us: shards(): lax.all_gather(right_factor, 'fsdp', axis=0, tiled=True)]
    another operation x9 -> x0, other arithmetic: 54.3 us -> none  [the longest x6 34 us: shards(): lower_factor = jnp.linalg.cholesky(gram_matrix)]
    reduce_scatter x1 -> x0, waiting for transfers between devices: 36.2 us -> none  [shards(): lax.psum_scatter(lax.dot_general(columns, orthonormal, (((0,), (0,)), (()...]
    another operation x5 -> x0, matrix products: 6.55 us -> none  [the longest x3 6.08 us: shards(): jax.scipy.linalg.solve_triangular(lower_factor, projected.T, lower=True)]
  transfers between devices with their start and end apart: 6 -> 0, of which waited for: 6 -> 0; matrix products, arithmetic and copies ran while one was open for 0% -> 0% of each run, Pallas kernels for 0% -> 0%
where the time goes in v1:
time: 224 us; the launch traced here: 223 us
  Pallas kernels  220 us (98%)
    pallas_call x1, Pallas kernels, by_kernels(): pl.pallas_call(functools.partial(orthonormalize, reps, shard_n), out_shap...  83.2 us
    pallas_call x1, Pallas kernels, by_kernels(): pl.pallas_call(functools.partial(sum_factor, reps, shard_n), out_shape=ja...  43 us
    pallas_call x1, Pallas kernels, by_kernels(): pl.pallas_call(functools.partial(gather_right, shard_n), out_shape=jax.Sh...  29.8 us
    pallas_call x1, Pallas kernels, by_kernels(): pl.pallas_call(functools.partial(finish, math.sqrt(total_rows * cols / ra...  27.6 us
    pallas_call x1, Pallas kernels, by_kernels(): pl.pallas_call(factor_term, grid=(steps,), out_shape=jax.ShapeDtypeStruct...  18.9 us
    pallas_call x1, Pallas kernels, by_kernels(): pl.pallas_call(project, grid=(steps,), out_shape=jax.ShapeDtypeStruct((ro...  17.9 us

profile of v1, /device:TPU:0, one launch (start us, length us, event | category | flops | bytes accessed | tf_op | source)
XLA Modules:
  0.0 223.0 jit_solution(6353768038536106977)
XLA Ops:
  0.6 29.8 %gather_right.1.right_ref = f32[2304,256]{1,0:T(8,128)} custom-call(f32[288,256]{1,0:T(8,128)} %own_ref.1), custom_call_target="tpu_custom_call" | custom-call | tf_op jit(solution)/shard_map/gather_right/pallas_call | solution.py:372
  30.4 17.9 %project.1.part_ref = f32[2304,256]{1,0:T(8,128)} custom-call(f32[1,2304,2304]{2,1,0:T(8,128)} %m_ref.5, bf16[1,2304,2304]{2,1,0:T(8,128)(2,1)} %g_ref.5, f32[2304,256]{1,0:T(8,128)} %gather_right.1.right_ref), custom_call_target="tpu_custom_call" | custom-call | tf_op jit(solution)/shard_map/project/pallas_call | solution.py:380
  48.3 83.2 %orthonormalize.1.q_ref = f32[2304,256]{1,0:T(8,128)} custom-call(f32[2304,256]{1,0:T(8,128)} %project.1.part_ref), custom_call_target="tpu_custom_call" | custom-call | tf_op jit(solution)/shard_map/orthonormalize/pallas_call | solution.py:389
  131.5 18.9 %factor_term.1.part_ref = f32[256,2304]{1,0:T(8,128)} custom-call(f32[1,2304,2304]{2,1,0:T(8,128)} %m_ref.5, bf16[1,2304,2304]{2,1,0:T(8,128)(2,1)} %g_ref.5, f32[2304,256]{1,0:T(8,128)} %orthonormalize.1.q_ref), custom_call_target="tpu_custom_call" | custom-call | tf_op jit(solution)/shard_map/factor_term/pallas_call | solution.py:405
  150.4 43.0 %sum_factor.1.factor_ref = f32[256,2304]{1,0:T(8,128)} custom-call(f32[256,2304]{1,0:T(8,128)} %factor_term.1.part_ref), custom_call_target="tpu_custom_call" | custom-call | tf_op jit(solution)/shard_map/sum_factor/pallas_call | solution.py:413
  193.3 27.6 %finish.1 = (f32[1,2304,2304]{2,1,0:T(8,128)}, bf16[2304,2304]{1,0:T(8,128)(2,1)}, f32[256,2304]{1,0:T(8,128)}) custom-call(f32[1,2304,2304]{2,1,0:T(8,128)} %m_ref.5, bf16[1,2304,2304]{2,1,0:T(8,128)(2,1)} %g_ref.5, f32[2304,256]{1,0:T(8,128)} %orthonormalize.1.q_ref, f32[256,2304]{1,0:T(8,128)} %sum_factor.1.factor_ref), custom_call_target="tpu_custom_call" | custom-call | tf_op jit(solution)/shard_map/finish/pallas_call | solution.py:427
  220.9 1.2 dynamic-slice_bitcast_fusion
  222.1 0.9 copy.6

commit v2 on v1

--- a/solution.py
+++ b/solution.py
@@ -212,7 +212,7 @@
 def factor_term(m_ref, g_ref, q_ref, out_ref):
     bh, bl = split(m_ref[0] + g_ref[0].astype(f32))
     qh, ql = split(q_ref[...].T)
-    term = dot(qh, bh) + dot(qh, bl) + dot(ql, bh)
+    term = dot(jnp.concatenate([qh, qh, ql], axis=1), jnp.concatenate([bh, bl, bh], axis=0))
 
     @pl.when(pl.program_id(0) == 0)
     def _():
@@ -332,7 +332,7 @@
         copy.wait_send()
 
 
-def finish(scale, m_ref, g_ref, q_ref, factor_ref, mom_ref, upd_ref, new_ref, plain, high, low):
+def finish(scale, m_ref, g_ref, q_ref, factor_ref, mom_ref, upd_ref, new_ref, plain, pieces):
     @pl.when(pl.program_id(0) == 0)
     def _():
         factor = factor_ref[...]
@@ -340,11 +340,12 @@
         new = factor / norms
         new_ref[...] = new
         plain[...] = ((1.0 - decay_rate) * factor).astype(bf16)
-        high[...], low[...] = split(new)
+        high, low = split(new)
+        pieces[...] = jnp.concatenate([high, low, high], axis=0)
 
     qh, ql = split(q_ref[...])
     mom_ref[0] = (m_ref[0] + g_ref[0].astype(f32)) - dot(qh, plain[...])
-    direction = dot(qh, high[...]) + dot(qh, low[...]) + dot(ql, high[...])
+    direction = dot(jnp.concatenate([qh, qh, ql], axis=1), pieces[...])
     upd_ref[...] = (scale * direction).astype(bf16)
 
 
@@ -434,7 +435,7 @@
         ),
         in_specs=[cube, cube, stripe(rank), fixed(rank, cols)],
         out_specs=(cube, stripe(cols), fixed(rank, cols)),
-        scratch_shapes=[pltpu.VMEM((rank, cols), bf16)] * 3,
+        scratch_shapes=[pltpu.VMEM((rank, cols), bf16), pltpu.VMEM((3 * rank, cols), bf16)],
         compiler_params=params(), name="finish",
     )(momentum, gradient, orthonormal, factor)
     own = cols // shard_n

time: 224 us -> 224 us (level)
  no operation moved by 1% of the time
where the time goes in v2:
time: 224 us; the launch traced here: 223 us
  Pallas kernels  220 us (98%)
    pallas_call x1, Pallas kernels, by_kernels(): pl.pallas_call(functools.partial(orthonormalize, reps, shard_n), out_shap...  83.2 us
    pallas_call x1, Pallas kernels, by_kernels(): pl.pallas_call(functools.partial(sum_factor, reps, shard_n), out_shape=ja...  43 us
    pallas_call x1, Pallas kernels, by_kernels(): pl.pallas_call(functools.partial(gather_right, shard_n), out_shape=jax.Sh...  29.8 us
    pallas_call x1, Pallas kernels, by_kernels(): pl.pallas_call(functools.partial(finish, math.sqrt(total_rows * cols / ra...  27.6 us
    pallas_call x1, Pallas kernels, by_kernels(): pl.pallas_call(factor_term, grid=(steps,), out_shape=jax.ShapeDtypeStruct...  18.6 us
    pallas_call x1, Pallas kernels, by_kernels(): pl.pallas_call(project, grid=(steps,), out_shape=jax.ShapeDtypeStruct((ro...  17.9 us

profile of v2, /device:TPU:0, one launch (start us, length us, event | category | flops | bytes accessed | tf_op | source)
XLA Modules:
  0.0 222.7 jit_solution(7768278734845446633)
XLA Ops:
  0.6 29.8 %gather_right.1.right_ref = f32[2304,256]{1,0:T(8,128)} custom-call(f32[288,256]{1,0:T(8,128)} %own_ref.1), custom_call_target="tpu_custom_call" | custom-call | tf_op jit(solution)/shard_map/gather_right/pallas_call | solution.py:373
  30.4 17.9 %project.1.part_ref = f32[2304,256]{1,0:T(8,128)} custom-call(f32[1,2304,2304]{2,1,0:T(8,128)} %m_ref.5, bf16[1,2304,2304]{2,1,0:T(8,128)(2,1)} %g_ref.5, f32[2304,256]{1,0:T(8,128)} %gather_right.1.right_ref), custom_call_target="tpu_custom_call" | custom-call | tf_op jit(solution)/shard_map/project/pallas_call | solution.py:381
  48.3 83.2 %orthonormalize.1.q_ref = f32[2304,256]{1,0:T(8,128)} custom-call(f32[2304,256]{1,0:T(8,128)} %project.1.part_ref), custom_call_target="tpu_custom_call" | custom-call | tf_op jit(solution)/shard_map/orthonormalize/pallas_call | solution.py:390
  131.5 18.6 %factor_term.1.part_ref = f32[256,2304]{1,0:T(8,128)} custom-call(f32[1,2304,2304]{2,1,0:T(8,128)} %m_ref.5, bf16[1,2304,2304]{2,1,0:T(8,128)(2,1)} %g_ref.5, f32[2304,256]{1,0:T(8,128)} %orthonormalize.1.q_ref), custom_call_target="tpu_custom_call" | custom-call | tf_op jit(solution)/shard_map/factor_term/pallas_call | solution.py:406
  150.0 43.0 %sum_factor.1.factor_ref = f32[256,2304]{1,0:T(8,128)} custom-call(f32[256,2304]{1,0:T(8,128)} %factor_term.1.part_ref), custom_call_target="tpu_custom_call" | custom-call | tf_op jit(solution)/shard_map/sum_factor/pallas_call | solution.py:414
  193.0 27.6 %finish.1 = (f32[1,2304,2304]{2,1,0:T(8,128)}, bf16[2304,2304]{1,0:T(8,128)(2,1)}, f32[256,2304]{1,0:T(8,128)}) custom-call(f32[1,2304,2304]{2,1,0:T(8,128)} %m_ref.5, bf16[1,2304,2304]{2,1,0:T(8,128)(2,1)} %g_ref.5, f32[2304,256]{1,0:T(8,128)} %orthonormalize.1.q_ref, f32[256,2304]{1,0:T(8,128)} %sum_factor.1.factor_ref), custom_call_target="tpu_custom_call" | custom-call | tf_op jit(solution)/shard_map/finish/pallas_call | solution.py:428
  220.6 1.2 dynamic-slice_bitcast_fusion
  221.8 0.9 copy.6
